TPU v7x, 32 devices: a whole 2x2x4 slice. The times are simulated.
32 devices in a mesh: rows: 8 (over z, x), cols: 4 (over y, core).
Axes of the slice: x: 2, y: 2, z: 4, core: 2. Of those that a mesh axis runs over, the one named last changes fastest.
Arguments:
- basis: bfloat16 [65536, 512], P('rows', 'cols'), may hold values from -6 to 6
- lower: bfloat16 [256, 256, 256], P('rows'), may hold values from -0.375 to 0.375
- diag: bfloat16 [256, 256, 256], P('rows'), may hold values from -0.375 to 0.375
- upper: bfloat16 [256, 256, 256], P('rows'), may hold values from -0.375 to 0.375
- inverse: bfloat16 [256, 256, 256], P('rows'), may hold values from -0.375 to 0.375
Outputs:
- ortho: bfloat16 [65536, 512], P('rows', 'cols')
- projected: float32 [512, 512], P(None, 'cols')
All inputs are finite; a program needn't handle non-finite values.
Results may differ from a plain program's by a relative error of at most 0.0085.
Values may be sent and summed in bfloat16 or wider, within the bound.
A program may use at most 128 MiB of HBM per device.

v0:
```python
import jax
import jax.numpy as jnp
from jax import lax
from jax.sharding import PartitionSpec as P


def extended(block, sides, width):
    for axis, dim in sides:
        count = lax.axis_size(axis)
        forward = [(i, i + 1) for i in range(count - 1)]
        backward = [(target, source) for source, target in forward]
        low = lax.ppermute(
            lax.slice_in_dim(block, block.shape[dim] - width, None, axis=dim), axis, forward
        )
        high = lax.ppermute(lax.slice_in_dim(block, 0, width, axis=dim), axis, backward)
        block = jnp.concatenate([low, block, high], axis=dim)
    return block


def inner(left, right):
    return lax.dot_general(
        left, right, (((0,), (0,)), ((), ())), preferred_element_type=jnp.float32
    )


def apply_blocks(padded, lower, diag, upper, inverse):
    count = diag.shape[0]
    size = diag.shape[1]
    width = padded.shape[1]
    blocks = padded.reshape(count + 2, size, width)
    mixed = jnp.einsum("bij,bjc->bic", lower, blocks[:-2], preferred_element_type=jnp.float32)
    mixed = mixed + jnp.einsum(
        "bij,bjc->bic", diag, blocks[1:-1], preferred_element_type=jnp.float32
    )
    mixed = mixed + jnp.einsum(
        "bij,bjc->bic", upper, blocks[2:], preferred_element_type=jnp.float32
    )
    mixed = mixed.astype(jnp.bfloat16)
    result = jnp.einsum("bij,bjc->bic", inverse, mixed, preferred_element_type=jnp.float32)
    return result.astype(jnp.bfloat16).reshape(count * size, width)


def inverse_upper(gram):
    factor = jnp.linalg.cholesky(gram)
    identity = jnp.eye(gram.shape[0], dtype=jnp.float32)
    linv = lax.linalg.triangular_solve(factor, identity, left_side=True, lower=True)
    return linv.T.astype(jnp.bfloat16)


def shards(basis, lower, diag, upper, inverse):
    size = diag.shape[1]
    width = basis.shape[1]

    def operate(field):
        padded = extended(field, (("rows", 0),), size)
        return apply_blocks(padded, lower, diag, upper, inverse)

    work = operate(basis)
    wide = lax.all_gather(work, "cols", axis=1, tiled=True)
    gram = lax.psum(inner(wide, wide), "rows")
    rinv = inverse_upper(gram)
    start = lax.axis_index("cols") * width
    ortho_all = jnp.dot(wide, rinv, preferred_element_type=jnp.float32).astype(jnp.bfloat16)
    ortho = lax.dynamic_slice_in_dim(ortho_all, start, width, 1)
    image = operate(ortho)
    projected = lax.psum(inner(ortho_all, image), "rows")
    return (ortho, projected)


def solution(mesh):
    in_specs = (
        P("rows", "cols"),
        P("rows", None, None),
        P("rows", None, None),
        P("rows", None, None),
        P("rows", None, None),
    )
    out_specs = (P("rows", "cols"), P(None, "cols"))
    return jax.shard_map(shards, mesh=mesh, in_specs=in_specs, out_specs=out_specs, check_vma=False)
```

profile of v0, /device:TPU:0, one launch (start us, length us, event | category | flops | bytes accessed | tf_op | source)
XLA Modules:
  0.0 457.5 jit_solution(3944854083608453380)
XLA Ops:
  9.4 5.5 %collective-permute-start = (bf16[256,128]{1,0:T(8,128)(2,1)S(1)}, bf16[256,128]{1,0:T(8,128)(2,1)S(1)}, u32[]{:S(2)}, u32[]{:S(2)}) collective-permute-start(bf16[256,128]{1,0:T(8,128)(2,1)S(1)} %get-tuple-element.27), channel_id=1, source_target_pairs={{0,4},{4,8},{8,12},{12,16},{16,20},{20,24},{24,28},{1,5},{5,9},{9,... | collective-permute-start | bytes 196616 | tf_op jit(solution)/shard_map/ppermute | solution.py:12
  14.9 6.5 %fusion.49 = f32[32,256,128]{1,2,0:T(8,128)} fusion(bf16[32,256,256]{2,1,0:T(8,128)(2,1)} %param.7, bf16[32,256,128]{2,1,0:T(8,128)(2,1)} %bitcast.98), kind=kOutput, calls=%fused_computation.97 | convolution fusion | flops 536870912 | bytes 10485760 | tf_op jit(solution)/shard_map/bij,bjc->bic/dot_general | solution.py:32
  23.6 3.5 fusion.48
  27.0 10.1 %convert_bitcast_fusion.1 = bf16[32,256,128]{1,2,0:T(8,128)(2,1)} fusion(bf16[32,256,256]{2,1,0:T(8,128)(2,1)} %param.9, f32[32,256,128]{1,2,0:T(8,128)} %fusion.49, f32[32,128,256]{2,1,0:T(8,128)} %fusion.48, bf16[32,256,128]{2,1,0:T(8,128)(2,1)S(1)} %bitcast.99, bf16[32,256,256]{2,1,0:T(8,128)(2,1)} %param.8), kind=kOutput, calls=%fused_computation.14 | convolution fusion | flops 1077936128 | bytes 20971520 | tf_op jit(solution)/shard_map/bij,bjc->bic/dot_general | solution.py:39
  37.1 4.0 copy.9
  41.2 61.1 %all-gather.2.cloned.1.call-done = bf16[8192,512]{1,0:T(8,128)(2,1)} async-done(((bf16[8192,128]{1,0:T(8,128)(2,1)}), bf16[8192,512]{1,0:T(8,128)(2,1)}) %all-gather.2.cloned.1.call-update) | async-done | bytes 8388624 | tf_op jit(solution)/shard_map/all_gather | solution.py:59
  102.4 11.3 %fusion.50 = f32[512,512]{0,1:T(8,128)} fusion(bf16[8192,512]{1,0:T(8,128)(2,1)} %all-gather.2.cloned.1.call-done), kind=kOutput, calls=%fused_computation.98 | convolution fusion | flops 4294967296 | bytes 9437184 | tf_op jit(solution)/shard_map/dot_general | solution.py:21
  114.8 77.2 %all-reduce.4.cloned.1.call-done = f32[512,512]{0,1:T(8,128)} async-done(((f32[512,512]{0,1:T(8,128)}), f32[512,512]{0,1:T(8,128)}) %all-reduce.4.cloned.1.call-update) | async-done | bytes 1048592 | tf_op jit(solution)/shard_map/psum | solution.py:60
  195.1 11.7 %cholesky.104 = f32[128,128]{1,0:T(8,128)S(1)} custom-call(f32[128,128]{1,0:T(8,128)S(1)} %cholesky.266), custom_call_target="Cholesky" | custom-call | tf_op jit(solution)/shard_map/jit(cholesky)/cholesky | solution.py:44
  206.8 9.8 %custom-call.30 = f32[1,128,128]{1,2,0:T(8,128)S(1)} custom-call(f32[1,128,128]{2,1,0:T(8,128)S(1)} %get-tuple-element.37), custom_call_target="InvertDiagBlocksLowerTriangular" | custom-call | tf_op jit(solution)/shard_map/jit(cholesky)/cholesky | solution.py:44
  217.4 11.7 %cholesky.217 = f32[128,128]{1,0:T(8,128)S(1)} custom-call(f32[128,128]{1,0:T(8,128)S(1)} %cholesky.270), custom_call_target="Cholesky" | custom-call | tf_op jit(solution)/shard_map/jit(cholesky)/cholesky | solution.py:44
  229.2 10.0 %custom-call.31 = f32[1,128,128]{1,2,0:T(8,128)S(1)} custom-call(f32[1,128,128]{2,1,0:T(8,128)S(1)} %get-tuple-element.34), custom_call_target="InvertDiagBlocksLowerTriangular" | custom-call | tf_op jit(solution)/shard_map/jit(cholesky)/cholesky | solution.py:44
  239.8 11.7 %cholesky.238 = f32[128,128]{1,0:T(8,128)S(1)} custom-call(f32[128,128]{1,0:T(8,128)S(1)} %cholesky.275), custom_call_target="Cholesky" | custom-call | tf_op jit(solution)/shard_map/jit(cholesky)/cholesky | solution.py:44
  252.3 9.8 %custom-call.32 = f32[1,128,128]{1,2,0:T(8,128)S(1)} custom-call(f32[1,128,128]{2,1,0:T(8,128)S(1)} %get-tuple-element.31), custom_call_target="InvertDiagBlocksLowerTriangular" | custom-call | tf_op jit(solution)/shard_map/jit(cholesky)/cholesky | solution.py:44
  262.7 11.7 %cholesky.255 = f32[128,128]{1,0:T(8,128)S(1)} custom-call(f32[128,128]{1,0:T(8,128)S(1)} %convolution_subtract_fusion.5), custom_call_target="Cholesky" | custom-call | tf_op jit(solution)/shard_map/jit(cholesky)/cholesky | solution.py:44
  278.9 10.8 %while.1 = (s32[]{:T(128)}, f32[512,512]{1,0:T(8,128)S(1)}, s32[4,2]{0,1:T(2,128)S(1)}, f32[4,128,128]{2,1,0:T(8,128)}, s32[]{:T(128)}) while((s32[]{:T(128)}, f32[512,512]{1,0:T(8,128)S(1)}, s32[4,2]{0,1:T(2,128)S(1)}, f32[4,128,128]{2,1,0:T(8,128)}, s32[]{:T(128)}) %tuple.38), condition=%wide.while_cond, body=%wide.while_body.sunk | while | flops 2 | bytes 132205 | solution.py:46
  289.7 40.1 %custom-call.33 = f32[4,128,128]{1,2,0:T(8,128)S(1)} custom-call(f32[4,128,128]{2,1,0:T(8,128)} %get-tuple-element.9), custom_call_target="InvertDiagBlocksLowerTriangular" | custom-call | tf_op jit(solution)/shard_map/triangular_solve | solution.py:46
  333.7 8.8 %convolution_convert_fusion = bf16[8192,512]{1,0:T(8,128)(2,1)S(1)} fusion(bf16[8192,512]{1,0:T(8,128)(2,1)} %all-gather.2.cloned.1.call-done, bf16[128,512]{1,0:T(8,128)(2,1)S(1)} %convolution_convert_fusion.1, bf16[128,512]{1,0:T(8,128)(2,1)S(1)} %get-tuple-element.40, bf16[128,512]{1,0:T(8,128)(2,1)S(1)} %get-tuple-element.42, ...), kind=kOutput, calls=%fused_computation.2 | convolution fusion | flops 4301258752 | bytes 17301504 | tf_op jit(solution)/shard_map/dot_general | solution.py:63
  342.9 3.6 collective-permute-start.2
  348.1 3.4 fusion.51
  353.7 3.5 fusion.52
  357.2 10.1 %convert_bitcast_fusion = bf16[32,256,128]{1,2,0:T(8,128)(2,1)} fusion(bf16[32,256,256]{2,1,0:T(8,128)(2,1)} %param.9, f32[32,128,256]{2,1,0:T(8,128)} %fusion.52, f32[32,128,256]{2,1,0:T(8,128)} %fusion.51, bf16[32,256,128]{2,1,0:T(8,128)(2,1)S(1)} %bitcast.100, bf16[32,256,256]{2,1,0:T(8,128)(2,1)} %param.6), kind=kOutput, calls=%fused_computation.13 | convolution fusion | flops 1077936128 | bytes 20971520 | tf_op jit(solution)/shard_map/bij,bjc->bic/dot_general | solution.py:39
  370.5 6.4 %fusion.53 = f32[512,128]{1,0:T(8,128)} fusion(bf16[8192,512]{1,0:T(8,128)(2,1)} %copy-done.5, bf16[8192,128]{1,0:T(8,128)(2,1)S(1)} %bitcast.104), kind=kOutput, calls=%fused_computation.101 | convolution fusion | flops 1073741824 | bytes 10747904 | tf_op jit(solution)/shard_map/dot_general | solution.py:21
  376.9 72.2 %all-reduce.6.cloned.1.call-done = f32[512,128]{1,0:T(8,128)} async-done(((f32[512,128]{1,0:T(8,128)}), f32[512,128]{1,0:T(8,128)}) %all-reduce.6.cloned.1.call-update) | async-done | bytes 262160 | tf_op jit(solution)/shard_map/psum | solution.py:66
  (75 shorter events, 36.9 us)
Async XLA Ops:
  7.2 95.2 %all-gather.2.cloned.1.call-start = ((), (), s32[]{:S(2)}) async-start(), calls=%async_computation | async-start | bytes 10485760 | tf_op jit(solution)/shard_map/all_gather | solution.py:59
  8.1 13.3 %collective-permute-start.1 = (bf16[256,128]{1,0:T(8,128)(2,1)S(1)}, bf16[256,128]{1,0:T(8,128)(2,1)S(1)}, u32[]{:S(2)}, u32[]{:S(2)}) collective-permute-start(bf16[256,128]{1,0:T(8,128)(2,1)S(1)} %get-tuple-element.26), channel_id=1, source_target_pairs={{4,0},{8,4},{12,8},{16,12},{20,16},{24,20},{28,24},{5,1},{9,5},{13... | collective-permute-start | bytes 196616 | tf_op jit(solution)/shard_map/ppermute | solution.py:15
  9.4 12.0 %collective-permute-start = (bf16[256,128]{1,0:T(8,128)(2,1)S(1)}, bf16[256,128]{1,0:T(8,128)(2,1)S(1)}, u32[]{:S(2)}, u32[]{:S(2)}) collective-permute-start(bf16[256,128]{1,0:T(8,128)(2,1)S(1)} %get-tuple-element.27), channel_id=1, source_target_pairs={{0,4},{4,8},{8,12},{12,16},{16,20},{20,24},{24,28},{1,5},{5,9},{9,... | collective-permute-start | bytes 196616 | tf_op jit(solution)/shard_map/ppermute | solution.py:12
  14.9 6.5 %copy-start.4 = (bf16[8192,128]{1,0:T(8,128)(2,1)S(1)}, bf16[8192,128]{1,0:T(8,128)(2,1)}, u32[]{:S(2)}) copy-start(bf16[8192,128]{1,0:T(8,128)(2,1)} %param.5) | copy-start | bytes 6291460
  21.4 2.2 copy-start.2
  41.2 150.9 %all-reduce.4.cloned.1.call-start = ((), (), s32[]{:S(2)}) async-start(), calls=%async_computation.1 | async-start | bytes 2097152 | tf_op jit(solution)/shard_map/psum | solution.py:60
  113.7 335.5 %all-reduce.6.cloned.1.call-start = ((), (), s32[]{:S(2)}) async-start(), calls=%async_computation.2 | async-start | bytes 524288 | tf_op jit(solution)/shard_map/psum | solution.py:66
  342.5 9.0 %copy-start.5 = (bf16[8192,512]{1,0:T(8,128)(2,1)}, bf16[8192,512]{1,0:T(8,128)(2,1)S(1)}, u32[]{:S(2)}) copy-start(bf16[8192,512]{1,0:T(8,128)(2,1)S(1)} %convolution_convert_fusion) | copy-start | bytes 25165828
  342.5 5.6 %copy-start.3 = (bf16[32,256,256]{2,1,0:T(8,128)(2,1)S(1)}, bf16[32,256,256]{2,1,0:T(8,128)(2,1)}, u32[]{:S(2)}) copy-start(bf16[32,256,256]{2,1,0:T(8,128)(2,1)} %param.7) | copy-start | bytes 12582916
  342.8 9.9 %copy-start = (bf16[8192,128]{1,0:T(8,128)(2,1)}, bf16[8192,128]{1,0:T(8,128)(2,1)S(1)}, u32[]{:S(2)}) copy-start(bf16[8192,128]{1,0:T(8,128)(2,1)S(1)} %constant_dynamic-slice_fusion.2) | copy-start | bytes 6291460
  342.9 8.7 %collective-permute-start.2 = (bf16[256,128]{1,0:T(8,128)(2,1)S(1)}, bf16[256,128]{1,0:T(8,128)(2,1)S(1)}, u32[]{:S(2)}, u32[]{:S(2)}) collective-permute-start(bf16[256,128]{1,0:T(8,128)(2,1)S(1)} %get-tuple-element.20), channel_id=1, source_target_pairs={{0,4},{4,8},{8,12},{12,16},{16,20},{20,24},{24,28},{1,5},{5,9},{9,... | collective-permute-start | bytes 196616 | tf_op jit(solution)/shard_map/ppermute | solution.py:12
  346.5 6.3 %collective-permute-start.3 = (bf16[256,128]{1,0:T(8,128)(2,1)S(1)}, bf16[256,128]{1,0:T(8,128)(2,1)S(1)}, u32[]{:S(2)}, u32[]{:S(2)}) collective-permute-start(bf16[256,128]{1,0:T(8,128)(2,1)S(1)} %get-tuple-element.21), channel_id=1, source_target_pairs={{4,0},{8,4},{12,8},{16,12},{20,16},{24,20},{28,24},{5,1},{9,5},{13... | collective-permute-start | bytes 196616 | tf_op jit(solution)/shard_map/ppermute | solution.py:15
  351.5 2.2 copy-start.1
Sparse Core Ops, SparseCore 0:
  41.3 61.0 all-gather.1
  113.8 78.2 all-reduce.3
  377.1 72.0 all-reduce.5
where the time goes:
time: 465 us; the launch traced here: 458 us
  waiting for transfers between devices  212 us (46%)
  other arithmetic  122 us (26%)
  matrix products  69.1 us (15%)
  local copies, waits for them, and re-layouts  25.2 us (5%)
  between operations  16.9 us (4%)
  starting transfers between devices  12.3 us (3%)
    another operation x14, other arithmetic, inverse_upper(): factor = jnp.linalg.cholesky(gram)  79 us
    psum x1, waiting for transfers between devices, shards(): gram = lax.psum(inner(wide, wide), 'rows')  77.2 us
    psum x1, waiting for transfers between devices, shards(): projected = lax.psum(inner(ortho_all, image), 'rows')  72.2 us
    all_gather x1, waiting for transfers between devices, shards(): wide = lax.all_gather(work, 'cols', axis=1, tiled=True)  61.1 us
    another operation x3, other arithmetic, inverse_upper(): lax.linalg.triangular_solve(factor, identity, left_side=True, lower=True)  40.3 us
    dot_general x2, matrix products, apply_blocks(): jnp.einsum('bij,bjc->bic', inverse, mixed, preferred_element_type=jnp.flo...  20.1 us
    dot_general x2, matrix products, inner(): lax.dot_general(left, right, (((0,), (0,)), ((), ())), preferred_element_...  17.7 us
    another operation x12, local copies, waits for them, and re-layouts  10.8 us
  transfers between devices with their start and end apart: 7, of which 4 were waited for; matrix products, arithmetic and copies ran while one was open for 2% of the time, Pallas kernels for 0%

commit v1 on v0

--- a/solution.py
+++ b/solution.py
@@ -57,7 +57,7 @@
 
     work = operate(basis)
     wide = lax.all_gather(work, "cols", axis=1, tiled=True)
-    gram = lax.psum(inner(wide, wide), "rows")
+    gram = jnp.sum(lax.all_gather(inner(wide, wide), "rows"), axis=0)
     rinv = inverse_upper(gram)
     start = lax.axis_index("cols") * width
     ortho_all = jnp.dot(wide, rinv, preferred_element_type=jnp.float32).astype(jnp.bfloat16)

time: 465 us -> 515 us (1.11)
  waiting for transfers between devices: 212 us -> 258 us
    all_gather x0 -> x1, waiting for transfers between devices: none -> 124 us  [shards(): gram = jnp.sum(lax.all_gather(inner(wide, wide), 'rows'), axis=0)]
    psum x1 -> x0, waiting for transfers between devices: 77.2 us -> none  [shards(): gram = lax.psum(inner(wide, wide), 'rows')]
where the time goes in v1:
time: 515 us; the launch traced here: 509 us
  waiting for transfers between devices  258 us (50%)
  other arithmetic  125 us (24%)
  matrix products  72 us (14%)
  local copies, waits for them, and re-layouts  25.5 us (5%)
  between operations  16.9 us (3%)
  starting transfers between devices  11.7 us (2%)
    all_gather x1, waiting for transfers between devices, shards(): gram = jnp.sum(lax.all_gather(inner(wide, wide), 'rows'), axis=0)  124 us
    another operation x14, other arithmetic, inverse_upper(): factor = jnp.linalg.cholesky(gram)  79.1 us
    psum x1, waiting for transfers between devices, shards(): projected = lax.psum(inner(ortho_all, image), 'rows')  71.7 us
    all_gather x1, waiting for transfers between devices, shards(): wide = lax.all_gather(work, 'cols', axis=1, tiled=True)  61.1 us
    another operation x3, other arithmetic, inverse_upper(): lax.linalg.triangular_solve(factor, identity, left_side=True, lower=True)  40.3 us
    dot_general x2, matrix products, apply_blocks(): jnp.einsum('bij,bjc->bic', inverse, mixed, preferred_element_type=jnp.flo...  20.2 us
    dot_general x2, matrix products, inner(): lax.dot_general(left, right, (((0,), (0,)), ((), ())), preferred_element_...  17.7 us
    another operation x12, local copies, waits for them, and re-layouts  10.5 us
  transfers between devices with their start and end apart: 7, of which 4 were waited for; matrix products, arithmetic and copies ran while one was open for 2% of the time, Pallas kernels for 0%

profile of v1, /device:TPU:0, one launch (start us, length us, event | category | flops | bytes accessed | tf_op | source)
XLA Modules:
  0.0 508.7 jit_solution(17029540484713269794)
XLA Ops:
  9.4 5.5 %collective-permute-start = (bf16[256,128]{1,0:T(8,128)(2,1)S(1)}, bf16[256,128]{1,0:T(8,128)(2,1)S(1)}, u32[]{:S(2)}, u32[]{:S(2)}) collective-permute-start(bf16[256,128]{1,0:T(8,128)(2,1)S(1)} %get-tuple-element.27), channel_id=1, source_target_pairs={{0,4},{4,8},{8,12},{12,16},{16,20},{20,24},{24,28},{1,5},{5,9},{9,... | collective-permute-start | bytes 196616 | tf_op jit(solution)/shard_map/ppermute | solution.py:12
  14.9 6.4 %fusion.49 = f32[32,256,128]{1,2,0:T(8,128)} fusion(bf16[32,256,256]{2,1,0:T(8,128)(2,1)} %param.7, bf16[32,256,128]{2,1,0:T(8,128)(2,1)} %bitcast.99), kind=kOutput, calls=%fused_computation.97 | convolution fusion | flops 536870912 | bytes 10485760 | tf_op jit(solution)/shard_map/bij,bjc->bic/dot_general | solution.py:32
  23.6 3.5 fusion.48
  27.0 10.1 %convert_bitcast_fusion.1 = bf16[32,256,128]{1,2,0:T(8,128)(2,1)} fusion(bf16[32,256,256]{2,1,0:T(8,128)(2,1)} %param.9, f32[32,256,128]{1,2,0:T(8,128)} %fusion.49, f32[32,128,256]{2,1,0:T(8,128)} %fusion.48, bf16[32,256,128]{2,1,0:T(8,128)(2,1)S(1)} %bitcast.100, bf16[32,256,256]{2,1,0:T(8,128)(2,1)} %param.8), kind=kOutput, calls=%fused_computation.14 | convolution fusion | flops 1077936128 | bytes 20971520 | tf_op jit(solution)/shard_map/bij,bjc->bic/dot_general | solution.py:39
  37.1 4.0 copy.20
  41.2 61.1 %all-gather.4.cloned.1.call-done = bf16[8192,512]{1,0:T(8,128)(2,1)} async-done(((bf16[8192,128]{1,0:T(8,128)(2,1)}), bf16[8192,512]{1,0:T(8,128)(2,1)}) %all-gather.4.cloned.1.call-update) | async-done | bytes 8388624 | tf_op jit(solution)/shard_map/all_gather | solution.py:59
  102.4 11.2 %fusion.50 = f32[512,512]{1,0:T(8,128)} fusion(bf16[8192,512]{1,0:T(8,128)(2,1)} %all-gather.4.cloned.1.call-done), kind=kOutput, calls=%fused_computation.98 | convolution fusion | flops 4294967296 | bytes 9437184 | tf_op jit(solution)/shard_map/dot_general | solution.py:21
  114.1 124.2 %all-gather.6.cloned.1.call-done = f32[4096,512]{1,0:T(8,128)} async-done(((f32[512,512]{1,0:T(8,128)}), f32[4096,512]{1,0:T(8,128)}) %all-gather.6.cloned.1.call-update) | async-done | bytes 8388624 | tf_op jit(solution)/shard_map/all_gather | solution.py:60
  238.3 4.5 reduce_sum.9
  244.3 11.7 %cholesky.104 = f32[128,128]{1,0:T(8,128)S(1)} custom-call(f32[128,128]{1,0:T(8,128)S(1)} %cholesky.266), custom_call_target="Cholesky" | custom-call | tf_op jit(solution)/shard_map/jit(cholesky)/cholesky | solution.py:44
  256.2 9.8 %custom-call.30 = f32[1,128,128]{1,2,0:T(8,128)S(1)} custom-call(f32[1,128,128]{2,1,0:T(8,128)S(1)} %get-tuple-element.37), custom_call_target="InvertDiagBlocksLowerTriangular" | custom-call | tf_op jit(solution)/shard_map/jit(cholesky)/cholesky | solution.py:44
  268.5 11.9 %cholesky.217 = f32[128,128]{1,0:T(8,128)S(1)} custom-call(f32[128,128]{1,0:T(8,128)S(1)} %cholesky.270), custom_call_target="Cholesky" | custom-call | tf_op jit(solution)/shard_map/jit(cholesky)/cholesky | solution.py:44
  280.5 9.8 %custom-call.31 = f32[1,128,128]{1,2,0:T(8,128)S(1)} custom-call(f32[1,128,128]{2,1,0:T(8,128)S(1)} %get-tuple-element.34), custom_call_target="InvertDiagBlocksLowerTriangular" | custom-call | tf_op jit(solution)/shard_map/jit(cholesky)/cholesky | solution.py:44
  291.9 11.7 %cholesky.238 = f32[128,128]{1,0:T(8,128)S(1)} custom-call(f32[128,128]{1,0:T(8,128)S(1)} %cholesky.275), custom_call_target="Cholesky" | custom-call | tf_op jit(solution)/shard_map/jit(cholesky)/cholesky | solution.py:44
  304.3 9.8 %custom-call.32 = f32[1,128,128]{1,2,0:T(8,128)S(1)} custom-call(f32[1,128,128]{2,1,0:T(8,128)S(1)} %get-tuple-element.31), custom_call_target="InvertDiagBlocksLowerTriangular" | custom-call | tf_op jit(solution)/shard_map/jit(cholesky)/cholesky | solution.py:44
  315.6 12.1 %cholesky.255 = f32[128,128]{1,0:T(8,128)S(1)} custom-call(f32[128,128]{1,0:T(8,128)S(1)} %convolution_subtract_fusion.5), custom_call_target="Cholesky" | custom-call | tf_op jit(solution)/shard_map/jit(cholesky)/cholesky | solution.py:44
  331.8 10.6 %while.1 = (s32[]{:T(128)}, f32[512,512]{1,0:T(8,128)S(1)}, s32[4,2]{0,1:T(2,128)S(1)}, f32[4,128,128]{2,1,0:T(8,128)}, s32[]{:T(128)}) while((s32[]{:T(128)}, f32[512,512]{1,0:T(8,128)S(1)}, s32[4,2]{0,1:T(2,128)S(1)}, f32[4,128,128]{2,1,0:T(8,128)}, s32[]{:T(128)}) %tuple.38), condition=%wide.while_cond, body=%wide.while_body.sunk | while | flops 2 | bytes 132205 | solution.py:46
  342.4 40.1 %custom-call.33 = f32[4,128,128]{1,2,0:T(8,128)S(1)} custom-call(f32[4,128,128]{2,1,0:T(8,128)} %get-tuple-element.9), custom_call_target="InvertDiagBlocksLowerTriangular" | custom-call | tf_op jit(solution)/shard_map/triangular_solve | solution.py:46
  385.5 8.8 %convolution_convert_fusion = bf16[8192,512]{1,0:T(8,128)(2,1)S(1)} fusion(bf16[8192,512]{1,0:T(8,128)(2,1)} %all-gather.4.cloned.1.call-done, bf16[128,512]{1,0:T(8,128)(2,1)S(1)} %convolution_convert_fusion.1, bf16[128,512]{1,0:T(8,128)(2,1)S(1)} %get-tuple-element.40, bf16[128,512]{1,0:T(8,128)(2,1)S(1)} %get-tuple-element.42, ...), kind=kOutput, calls=%fused_computation.2 | convolution fusion | flops 4301258752 | bytes 17301504 | tf_op jit(solution)/shard_map/dot_general | solution.py:63
  399.7 3.5 fusion.51
  405.4 3.5 fusion.52
  408.8 10.1 %convert_bitcast_fusion = bf16[32,256,128]{1,2,0:T(8,128)(2,1)} fusion(bf16[32,256,256]{2,1,0:T(8,128)(2,1)} %param.9, f32[32,128,256]{2,1,0:T(8,128)} %fusion.52, f32[32,128,256]{2,1,0:T(8,128)} %fusion.51, bf16[32,256,128]{2,1,0:T(8,128)(2,1)S(1)} %bitcast.101, bf16[32,256,256]{2,1,0:T(8,128)(2,1)} %param.6), kind=kOutput, calls=%fused_computation.13 | convolution fusion | flops 1077936128 | bytes 20971520 | tf_op jit(solution)/shard_map/bij,bjc->bic/dot_general | solution.py:39
  422.1 6.4 %fusion.53 = f32[512,128]{1,0:T(8,128)} fusion(bf16[8192,512]{1,0:T(8,128)(2,1)} %copy-done.6, bf16[8192,128]{1,0:T(8,128)(2,1)S(1)} %bitcast.106), kind=kOutput, calls=%fused_computation.101 | convolution fusion | flops 1073741824 | bytes 10747904 | tf_op jit(solution)/shard_map/dot_general | solution.py:21
  428.6 71.7 %all-reduce.3.cloned.1.call-done = f32[512,128]{1,0:T(8,128)} async-done(((f32[512,128]{1,0:T(8,128)}), f32[512,128]{1,0:T(8,128)}) %all-reduce.3.cloned.1.call-update) | async-done | bytes 262160 | tf_op jit(solution)/shard_map/psum | solution.py:66
  (78 shorter events, 40.3 us)
Async XLA Ops:
  7.2 95.2 %all-gather.4.cloned.1.call-start = ((), (), s32[]{:S(2)}) async-start(), calls=%async_computation | async-start | bytes 10485760 | tf_op jit(solution)/shard_map/all_gather | solution.py:59
  8.1 13.3 %collective-permute-start.1 = (bf16[256,128]{1,0:T(8,128)(2,1)S(1)}, bf16[256,128]{1,0:T(8,128)(2,1)S(1)}, u32[]{:S(2)}, u32[]{:S(2)}) collective-permute-start(bf16[256,128]{1,0:T(8,128)(2,1)S(1)} %get-tuple-element.26), channel_id=1, source_target_pairs={{4,0},{8,4},{12,8},{16,12},{20,16},{24,20},{28,24},{5,1},{9,5},{13... | collective-permute-start | bytes 196616 | tf_op jit(solution)/shard_map/ppermute | solution.py:15
  9.4 12.0 %collective-permute-start = (bf16[256,128]{1,0:T(8,128)(2,1)S(1)}, bf16[256,128]{1,0:T(8,128)(2,1)S(1)}, u32[]{:S(2)}, u32[]{:S(2)}) collective-permute-start(bf16[256,128]{1,0:T(8,128)(2,1)S(1)} %get-tuple-element.27), channel_id=1, source_target_pairs={{0,4},{4,8},{8,12},{12,16},{16,20},{20,24},{24,28},{1,5},{5,9},{9,... | collective-permute-start | bytes 196616 | tf_op jit(solution)/shard_map/ppermute | solution.py:12
  14.9 6.5 %copy-start.4 = (bf16[8192,128]{1,0:T(8,128)(2,1)S(1)}, bf16[8192,128]{1,0:T(8,128)(2,1)}, u32[]{:S(2)}) copy-start(bf16[8192,128]{1,0:T(8,128)(2,1)} %param.5) | copy-start | bytes 6291460
  21.4 2.2 copy-start.2
  41.2 197.1 %all-gather.6.cloned.1.call-start = ((), (), s32[]{:S(2)}) async-start(), calls=%async_computation.2 | async-start | bytes 9437184 | tf_op jit(solution)/shard_map/all_gather | solution.py:60
  113.6 386.7 %all-reduce.3.cloned.1.call-start = ((), (), s32[]{:S(2)}) async-start(), calls=%async_computation.1 | async-start | bytes 524288 | tf_op jit(solution)/shard_map/psum | solution.py:66
  243.3 1.0 copy-start.5
  394.4 8.8 %copy-start.6 = (bf16[8192,512]{1,0:T(8,128)(2,1)}, bf16[8192,512]{1,0:T(8,128)(2,1)S(1)}, u32[]{:S(2)}) copy-start(bf16[8192,512]{1,0:T(8,128)(2,1)S(1)} %convolution_convert_fusion) | copy-start | bytes 25165828
  394.4 5.3 %copy-start.3 = (bf16[32,256,256]{2,1,0:T(8,128)(2,1)S(1)}, bf16[32,256,256]{2,1,0:T(8,128)(2,1)}, u32[]{:S(2)}) copy-start(bf16[32,256,256]{2,1,0:T(8,128)(2,1)} %param.7) | copy-start | bytes 12582916
  394.7 9.3 %copy-start = (bf16[8192,128]{1,0:T(8,128)(2,1)}, bf16[8192,128]{1,0:T(8,128)(2,1)S(1)}, u32[]{:S(2)}) copy-start(bf16[8192,128]{1,0:T(8,128)(2,1)S(1)} %constant_dynamic-slice_fusion.2) | copy-start | bytes 6291460
  394.7 8.5 %collective-permute-start.2 = (bf16[256,128]{1,0:T(8,128)(2,1)S(1)}, bf16[256,128]{1,0:T(8,128)(2,1)S(1)}, u32[]{:S(2)}, u32[]{:S(2)}) collective-permute-start(bf16[256,128]{1,0:T(8,128)(2,1)S(1)} %get-tuple-element.20), channel_id=1, source_target_pairs={{0,4},{4,8},{8,12},{12,16},{16,20},{20,24},{24,28},{1,5},{5,9},{9,... | collective-permute-start | bytes 196616 | tf_op jit(solution)/shard_map/ppermute | solution.py:12
  397.6 6.4 %collective-permute-start.3 = (bf16[256,128]{1,0:T(8,128)(2,1)S(1)}, bf16[256,128]{1,0:T(8,128)(2,1)S(1)}, u32[]{:S(2)}, u32[]{:S(2)}) collective-permute-start(bf16[256,128]{1,0:T(8,128)(2,1)S(1)} %get-tuple-element.21), channel_id=1, source_target_pairs={{4,0},{8,4},{12,8},{16,12},{20,16},{24,20},{28,24},{5,1},{9,5},{13... | collective-permute-start | bytes 196616 | tf_op jit(solution)/shard_map/ppermute | solution.py:15
  403.2 2.2 copy-start.1
Sparse Core Ops, SparseCore 0:
  41.3 61.0 all-gather.3
  113.8 124.4 all-gather.5
  428.7 71.5 all-reduce.2
